TPU v7x, 256 devices: a whole 4x4x8 slice. The times are simulated.
256 devices in a mesh: rep: 4 (over y), row: 4 (over z_hi), col: 16 (over z_lo, x, core).
Axes of the slice: x: 4, y: 4, z: 8 (z_hi: 4, z_lo: 2; z = z_hi * 2 + z_lo), core: 2. Of those that a mesh axis runs over, the one named last changes fastest.
Arguments:
- patches: bfloat16 [4096, 588], P(('rep', 'col')), may hold values from -20 to 20
- embed_weight: bfloat16 [588, 6144], P(None, 'row'), may hold values from -1 to 1
- embed_bias: float32 [6144], P('row'), may hold values from -3 to 3
- old_in: bfloat16 [64, 768, 1536], P(('row', 'col')), may hold values from -0.078125 to 0.078125
- old_out: bfloat16 [64, 1536, 768], P(('row', 'col')), may hold values from -0.0546875 to 0.0546875
- restore_id: int32 [1], replicated, may hold values from 0 to 47
- norm_gains: float32 [48, 6144], P(None, 'row'), may hold values from 0.1 to 1.9
- in_biases: float32 [48, 12288], P(None, 'col'), may hold values from -3 to 3
- out_biases: float32 [48, 6144], P(None, 'row'), may hold values from -3 to 3
- final_gain: float32 [6144], P('row'), may hold values from 0.1 to 1.9
- check_weight: bfloat16 [6144, 128], P('row'), may hold values from -0.078125 to 0.078125
Outputs:
- in_weight: bfloat16 [6144, 12288], P('row', 'col')
- out_weight: bfloat16 [12288, 6144], P('col', 'row')
- check_logits: float32 [4096, 128], P(('rep', 'col'))
All inputs are finite; a program needn't handle non-finite values.
Results may differ from a plain program's by a relative error of at most 0.0062.
Values may be sent and summed in bfloat16 or wider, within the bound.
A program may use at most 64 MiB of HBM per device.

v0:
```python
import jax
import jax.numpy as jnp
from jax import lax
from jax.sharding import PartitionSpec as P

EPSILON = 1e-06


def from_everyone(shard, axis):
    size = lax.axis_size(axis)
    return lax.all_to_all(
        jnp.broadcast_to(shard[None], (size, *shard.shape)), axis, 0, 0, tiled=True
    )


def taken_together(shard, axis):
    return from_everyone(shard, axis).sum(axis=0)


def packed_total(arrays, axis):
    ends = [0]
    for a in arrays:
        ends.append(ends[-1] + a.size)
    so_far = taken_together(jnp.concatenate([a.ravel() for a in arrays]), axis)
    return tuple((so_far[b:e].reshape(a.shape) for a, b, e in zip(arrays, ends, ends[1:])))


def for_sending(shard):
    return jax.tree.map(lambda a: a.astype(jnp.bfloat16) if a.dtype == jnp.float32 else a, shard)


def partner(value, axis, bit):
    mask = 2**bit
    pairs = [(source, source ^ mask) for source in range(lax.axis_size(axis))]
    return lax.ppermute(value, axis, pairs)


def rows_first(arrays, axis, dims):
    turned = [jnp.moveaxis(a, dim, 0) for a, dim in zip(arrays, dims)]
    widths = [t[0].size for t in turned]
    both = jnp.concatenate([t.reshape(-1, w) for t, w in zip(turned, widths)], axis=1)
    out = lax.all_gather(both, axis, axis=0, tiled=True)
    parts = jnp.split(out, [sum(widths[:k]) for k in range(1, len(widths))], axis=1)
    return tuple(
        (
            jnp.moveaxis(b.reshape(-1, *t.shape[1:]), 0, dim)
            for b, t, dim in zip(parts, turned, dims)
        )
    )


def cut_along(shard, dim, size):
    before, after = (shard.shape[:dim], shard.shape[dim + 1 :])
    return jnp.moveaxis(shard.reshape(*before, size, -1, *after), dim, 0)


def sent_and_summed(shard, axis, dim):
    size = lax.axis_size(axis)
    parts = lax.all_to_all(cut_along(shard, dim, size), axis, 0, 0, tiled=True)
    return jnp.sum(parts.astype(jnp.float32), axis=0)


def laid_out(parts, dim):
    shape = list(parts.shape[1:])
    shape[dim] *= parts.shape[0]
    return jnp.moveaxis(parts, 0, dim).reshape(shape)


def gathered_copies(shard, axis, dim):
    parts = from_everyone(shard, axis)
    return laid_out(parts, dim)


def pick_rows(restore_id, param_table):
    selector = (
        jnp.arange(param_table.shape[0], dtype=jnp.int32)[None, :] == restore_id[:, None]
    ).astype(jnp.float32)
    return jnp.dot(selector, param_table, precision=lax.Precision.HIGHEST)[0]


def norm_rows(values, gain_row):
    feature_count = values.shape[1] * lax.axis_size("row")
    totals = packed_total((jnp.sum(values, axis=1), jnp.sum(values * values, axis=1)), "row")
    average = totals[0][:, None] / feature_count
    spread = totals[1][:, None] / feature_count - average * average
    return ((values - average) * lax.rsqrt(spread + EPSILON) * gain_row).astype(jnp.bfloat16)


def move_halves(pieces, bit_total, device_index, exchange):
    for bit_number in range(bit_total):
        upper_side = device_index >> bit_number & 1 == 1
        outgoing = tuple(
            (jnp.where(upper_side, lower_part, upper_part) for lower_part, upper_part in pieces)
        )
        incoming = exchange(outgoing, bit_number)
        pieces = tuple(
            (
                (
                    jnp.where(upper_side, arrived, lower_part),
                    jnp.where(upper_side, upper_part, arrived),
                )
                for (lower_part, upper_part), arrived in zip(pieces, incoming)
            )
        )
    return pieces


def on_device(
    patches,
    embed_weight,
    embed_bias,
    old_in,
    old_out,
    restore_id,
    norm_gains,
    in_biases,
    out_biases,
    final_gain,
    check_weight,
):
    tiles_here, tile_rows, tile_cols = old_in.shape
    local_cols = tiles_here * tile_cols
    half_cols = local_cols // 2
    in_local = jnp.transpose(old_in, (1, 0, 2)).reshape(tile_rows, local_cols)
    out_local = old_out.reshape(local_cols, tile_rows)
    col_index = lax.axis_index("col")
    col_count = lax.axis_size("col")
    col_bits = col_count.bit_length() - 1
    share_rows = tile_rows // lax.axis_size("rep")
    first_row = lax.axis_index("rep") * share_rows
    in_share = lax.dynamic_slice_in_dim(in_local, first_row, share_rows, 0)
    out_share = lax.dynamic_slice_in_dim(out_local, first_row, share_rows, 1)
    pieces = (
        (in_share[:, :half_cols], in_share[:, half_cols:]),
        (out_share[:half_cols], out_share[half_cols:]),
    )
    pieces = move_halves(
        pieces,
        col_bits,
        col_index,
        lambda send_parts, bit_number: jax.tree.map(
            lambda part, own: part.astype(own.dtype),
            partner(for_sending(send_parts), "col", bit_number),
            send_parts,
        ),
    )
    gathered = rows_first(
        (pieces[0][0], pieces[0][1], pieces[1][0], pieces[1][1]), "rep", (0, 0, 1, 1)
    )
    in_weight = jnp.concatenate((gathered[0], gathered[1]), axis=0)
    out_weight = jnp.concatenate((gathered[2], gathered[3]), axis=1)
    layer_gain = pick_rows(restore_id, norm_gains)
    in_bias = pick_rows(restore_id, in_biases)
    out_bias = pick_rows(restore_id, out_biases)
    embedded = jnp.dot(patches, embed_weight, preferred_element_type=jnp.float32) + embed_bias
    normed = norm_rows(embedded, layer_gain)
    partial_pre = jnp.dot(
        lax.all_gather(normed, "col", axis=0, tiled=True),
        in_weight,
        preferred_element_type=jnp.float32,
    )
    pre_share = sent_and_summed(partial_pre.astype(jnp.bfloat16), "row", 0) + in_bias
    hidden = jax.nn.gelu(pre_share, approximate=False).astype(jnp.bfloat16)
    partial_branch = jnp.dot(
        gathered_copies(hidden, "row", 0), out_weight, preferred_element_type=jnp.float32
    )
    updated = embedded + sent_and_summed(partial_branch.astype(jnp.bfloat16), "col", 0) + out_bias
    final_normed = norm_rows(updated, final_gain)
    check_logits = lax.psum(
        jnp.dot(final_normed, check_weight, preferred_element_type=jnp.float32), "row"
    )
    return (in_weight, out_weight, check_logits)


def solution(mesh):
    placed = (
        P(("rep", "col"), None),
        P(None, "row"),
        P("row"),
        P(("row", "col"), None, None),
        P(("row", "col"), None, None),
        P(),
        P(None, "row"),
        P(None, "col"),
        P(None, "row"),
        P("row"),
        P("row", None),
    )
    return jax.shard_map(
        on_device,
        mesh=mesh,
        in_specs=placed,
        out_specs=(P("row", "col"), P("col", "row"), P(("rep", "col"), None)),
        check_vma=False,
    )
```

profile of v0, /device:TPU:6, one launch (start us, length us, event | category | flops | bytes accessed | tf_op | source)
XLA Modules:
  0.0 349.5 jit_solution(2980738248300091822)
XLA Ops:
  7.2 1.6 copy-done
  9.6 2.5 constant_dynamic-slice_fusion
  12.1 1.1 copy.25
  13.3 1.2 copy.26
  15.7 1.7 broadcast_select_fusion.12
  17.4 0.8 collective-permute-start.1
  18.2 1.7 broadcast_select_fusion.2
  20.0 1.2 collective-permute-start.5
  21.2 6.4 %collective-permute-done.1 = bf16[192,768]{1,0:T(8,128)(2,1)} collective-permute-done((bf16[192,768]{1,0:T(8,128)(2,1)}, bf16[192,768]{1,0:T(8,128)(2,1)}, u32[]{:S(2)}, u32[]{:S(2)}) %collective-permute-start.1) | collective-permute-done | bytes 294944 | tf_op jit(solution)/shard_map/ppermute | solution.py:35
  27.6 2.0 broadcast_select_fusion.15
  29.7 1.6 collective-permute-start.2
  31.3 2.7 collective-permute-done.5
  33.9 2.0 broadcast_select_fusion.5
  36.0 1.6 collective-permute-start.6
  37.6 4.3 %collective-permute-done.2 = bf16[192,768]{1,0:T(8,128)(2,1)} collective-permute-done((bf16[192,768]{1,0:T(8,128)(2,1)}, bf16[192,768]{1,0:T(8,128)(2,1)}, u32[]{:S(2)}, u32[]{:S(2)}) %collective-permute-start.2) | collective-permute-done | bytes 294944 | tf_op jit(solution)/shard_map/ppermute | solution.py:35
  41.9 1.1 broadcast_select_fusion.18
  43.1 4.2 %collective-permute-done.6 = bf16[768,192]{0,1:T(8,128)(2,1)} collective-permute-done((bf16[768,192]{0,1:T(8,128)(2,1)}, bf16[768,192]{0,1:T(8,128)(2,1)}, u32[]{:S(2)}, u32[]{:S(2)}) %collective-permute-start.6) | collective-permute-done | bytes 294944 | tf_op jit(solution)/shard_map/ppermute | solution.py:35
  47.2 1.1 broadcast_select_fusion.6
  48.6 1.5 collective-permute-done.3
  50.2 1.0 broadcast_select_fusion.17
  51.2 5.3 %collective-permute-done.7 = bf16[768,192]{0,1:T(8,128)(2,1)S(1)} collective-permute-done((bf16[768,192]{0,1:T(8,128)(2,1)S(1)}, bf16[768,192]{0,1:T(8,128)(2,1)S(1)}, u32[]{:S(2)}, u32[]{:S(2)}) %collective-permute-start.7) | collective-permute-done | bytes 294944 | tf_op jit(solution)/shard_map/ppermute | solution.py:35
  56.5 1.0 select_bitcast_fusion.1
  57.5 1.2 pad_maximum_fusion.2
  58.7 2.1 fusion.21
  61.5 6.1 %all-to-all-start = ((f32[4,1,128]{2,1,0:T(1,128)}), f32[4,1,128]{2,1,0:T(1,128)S(1)}, u32[]{:S(2)}, u32[]{:S(2)}) async-start(f32[4,1,128]{2,1,0:T(1,128)} %broadcast_in_dim.6), calls=%async_computation | async-start | bytes 4096 | tf_op jit(solution)/shard_map/all_to_all | solution.py:11
  68.5 6.7 %all-to-all-done = f32[4,1,128]{2,1,0:T(1,128)S(1)} async-done(((f32[4,1,128]{2,1,0:T(1,128)}), f32[4,1,128]{2,1,0:T(1,128)S(1)}, u32[]{:S(2)}, u32[]{:S(2)}) %all-to-all-start) | async-done | bytes 2080 | tf_op jit(solution)/shard_map/all_to_all | solution.py:11
  75.3 0.8 multiply_convert_fusion.1
  76.1 38.9 %all-gather.3.cloned.1.call-done = bf16[768,3072]{1,0:T(8,128)(2,1)} async-done(((bf16[192,3072]{1,0:T(8,128)(2,1)}), bf16[768,3072]{1,0:T(8,128)(2,1)}) %all-gather.3.cloned.1.call-update) | async-done | bytes 4718608 | tf_op jit(solution)/shard_map/all_gather | solution.py:42
  115.0 3.8 %slice_bitcast_fusion.1 = (bf16[768,768]{0,1:T(8,128)(2,1)S(1)}, bf16[768,768]{0,1:T(8,128)(2,1)}, bf16[768,768]{1,0:T(8,128)(2,1)S(1)}, bf16[768,768]{1,0:T(8,128)(2,1)S(1)}) fusion(bf16[768,3072]{1,0:T(8,128)(2,1)} %all-gather.3.cloned.1.call-done), kind=kLoop, calls=%fused_computation.9 | loop fusion | bytes 9437184 | tf_op jit(solution)/shard_map/transpose | solution.py:46
  118.8 1.6 pad_maximum_fusion
  120.3 34.0 %all-gather.5.cloned.1.call-done = bf16[1024,1536]{1,0:T(8,128)(2,1)} async-done(((bf16[64,1536]{1,0:T(8,128)(2,1)}), bf16[1024,1536]{1,0:T(8,128)(2,1)}) %all-gather.5.cloned.1.call-update) | async-done | bytes 3145744 | tf_op jit(solution)/shard_map/all_gather | solution.py:158
  154.3 6.4 %convolution_convert_fusion.1 = bf16[1024,768]{1,0:T(8,128)(2,1)} fusion(bf16[1024,1536]{1,0:T(8,128)(2,1)} %all-gather.5.cloned.1.call-done, bf16[1536,768]{1,0:T(8,128)(2,1)} %pad_maximum_fusion), kind=kOutput, calls=%fused_computation.6 | convolution fusion | flops 2416705536 | bytes 7077888 | tf_op jit(solution)/shard_map/dot_general | solution.py:157
  160.7 6.2 %all-to-all-start.1 = ((bf16[4,256,768]{2,1,0:T(8,128)(2,1)}), bf16[4,256,768]{2,1,0:T(8,128)(2,1)}, u32[]{:S(2)}, u32[]{:S(2)}) async-start(bf16[4,256,768]{2,1,0:T(8,128)(2,1)} %bitcast.54), calls=%async_computation.1 | async-start | bytes 3145728 | tf_op jit(solution)/shard_map/all_to_all | solution.py:59
  166.9 1.1 convolution_reduce_fusion.2
  168.0 28.4 %all-to-all-done.1 = bf16[4,256,768]{2,1,0:T(8,128)(2,1)} async-done(((bf16[4,256,768]{2,1,0:T(8,128)(2,1)}), bf16[4,256,768]{2,1,0:T(8,128)(2,1)}, u32[]{:S(2)}, u32[]{:S(2)}) %all-to-all-start.1) | async-done | bytes 1572896 | tf_op jit(solution)/shard_map/all_to_all | solution.py:59
  196.4 1.7 convert_reduce_fusion.1
  198.1 1.7 fusion.2
  199.9 50.6 %all_to_all.27 = bf16[4,256,768]{2,1,0:T(8,128)(2,1)S(1)} all-to-all(bf16[4,256,768]{2,1,0:T(8,128)(2,1)S(1)} %broadcast_in_dim.7), channel_id=1, replica_groups=mesh['rep'=4,'row'=4,'col'=16] {'row'}, dimensions={0} | all-to-all | bytes 3145728 | tf_op jit(solution)/shard_map/all_to_all | solution.py:11
  250.6 4.9 %convolution_convert_fusion = bf16[1024,1536]{1,0:T(8,128)(2,1)} fusion(bf16[1024,768]{1,0:T(8,128)(2,1)S(1)} %bitcast.55, bf16[768,768]{0,1:T(8,128)(2,1)S(1)} %copy-done.1, bf16[768,768]{0,1:T(8,128)(2,1)S(1)} %get-tuple-element.26), kind=kOutput, calls=%fused_computation.1 | convolution fusion | flops 2422210560 | bytes 7077888 | tf_op jit(solution)/shard_map/dot_general | solution.py:164
  255.5 6.5 %all-to-all-start.3 = ((bf16[16,64,1536]{2,1,0:T(8,128)(2,1)}), bf16[16,64,1536]{2,1,0:T(8,128)(2,1)}, u32[]{:S(2)}, u32[]{:S(2)}) async-start(bf16[16,64,1536]{2,1,0:T(8,128)(2,1)} %bitcast.53), calls=%async_computation.3 | async-start | bytes 6291456 | tf_op jit(solution)/shard_map/all_to_all | solution.py:59
  262.0 1.2 convolution_reduce_fusion
  263.2 43.8 %all-to-all-done.3 = bf16[16,64,1536]{2,1,0:T(8,128)(2,1)} async-done(((bf16[16,64,1536]{2,1,0:T(8,128)(2,1)}), bf16[16,64,1536]{2,1,0:T(8,128)(2,1)}, u32[]{:S(2)}, u32[]{:S(2)}) %all-to-all-start.3) | async-done | bytes 3145760 | tf_op jit(solution)/shard_map/all_to_all | solution.py:59
  307.0 2.4 convert_reduce_fusion
  309.4 0.9 fusion.20
  311.0 3.2 all-to-all-start.4
  314.2 2.8 pad_maximum_fusion.1
  317.1 4.3 %copy.23 = bf16[768,1536]{1,0:T(8,128)(2,1)} copy(bf16[768,1536]{0,1:T(8,128)(2,1)} %pad_maximum_fusion.1) | data formatting | bytes 4718592
  322.2 20.5 %psum.7 = f32[64,128]{1,0:T(8,128)} all-reduce(f32[64,128]{1,0:T(8,128)S(1)} %fusion.10), channel_id=1, replica_groups=mesh['rep'=4,'row'=4,'col'=16] {'row'}, use_global_device_ids=true, to_apply=%region_8.9 | all-reduce | flops 8192 | bytes 65536 | tf_op jit(solution)/shard_map/psum | solution.py:169
  (50 shorter events, 5.1 us)
Async XLA Ops:
  7.2 1.7 copy-start
  7.2 107.8 %all-gather.3.cloned.1.call-start = ((), (), s32[]{:S(2)}) async-start(), calls=%async_computation.5 | async-start | bytes 5898240 | tf_op jit(solution)/shard_map/all_gather | solution.py:42
  9.6 6.1 %collective-permute-start = (bf16[192,768]{1,0:T(8,128)(2,1)}, bf16[192,768]{1,0:T(8,128)(2,1)}, u32[]{:S(2)}, u32[]{:S(2)}) collective-permute-start(bf16[192,768]{1,0:T(8,128)(2,1)} %broadcast_select_fusion.9), channel_id=1, source_target_pairs={{0,1},{1,0},{2,3},{3,2},{4,5},{5,4},{6,7},{7,6},{8,9},{9,8},{10,11... | collective-permute-start | bytes 884744 | tf_op jit(solution)/shard_map/ppermute | solution.py:35
  15.2 3.1 collective-permute-start.4
  17.4 10.2 %collective-permute-start.1 = (bf16[192,768]{1,0:T(8,128)(2,1)}, bf16[192,768]{1,0:T(8,128)(2,1)}, u32[]{:S(2)}, u32[]{:S(2)}) collective-permute-start(bf16[192,768]{1,0:T(8,128)(2,1)} %broadcast_select_fusion.12), channel_id=1, source_target_pairs={{0,2},{1,3},{2,0},{3,1},{4,6},{5,7},{6,4},{7,5},{8,10},{9,11},{10,... | collective-permute-start | bytes 884744 | tf_op jit(solution)/shard_map/ppermute | solution.py:35
  20.0 14.0 %collective-permute-start.5 = (bf16[768,192]{0,1:T(8,128)(2,1)}, bf16[768,192]{0,1:T(8,128)(2,1)}, u32[]{:S(2)}, u32[]{:S(2)}) collective-permute-start(bf16[768,192]{0,1:T(8,128)(2,1)} %broadcast_select_fusion.2), channel_id=1, source_target_pairs={{0,2},{1,3},{2,0},{3,1},{4,6},{5,7},{6,4},{7,5},{8,10},{9,11},{10,... | collective-permute-start | bytes 884744 | tf_op jit(solution)/shard_map/ppermute | solution.py:35
  29.6 20.5 %copy-start.4 = (bf16[192,768]{1,0:T(8,128)(2,1)S(1)}, bf16[192,768]{1,0:T(8,128)(2,1)}, u32[]{:S(2)}) copy-start(bf16[192,768]{1,0:T(8,128)(2,1)} %get-tuple-element.21) | copy-start | bytes 884740
  29.6 20.5 %copy-start.5 = (bf16[192,768]{1,0:T(8,128)(2,1)S(1)}, bf16[192,768]{1,0:T(8,128)(2,1)}, u32[]{:S(2)}) copy-start(bf16[192,768]{1,0:T(8,128)(2,1)} %get-tuple-element.22) | copy-start | bytes 884740
  29.7 12.2 %collective-permute-start.2 = (bf16[192,768]{1,0:T(8,128)(2,1)}, bf16[192,768]{1,0:T(8,128)(2,1)}, u32[]{:S(2)}, u32[]{:S(2)}) collective-permute-start(bf16[192,768]{1,0:T(8,128)(2,1)} %get-tuple-element.20), channel_id=1, source_target_pairs={{0,4},{1,5},{2,6},{3,7},{4,0},{5,1},{6,2},{7,3},{8,12},{9,13},{10,... | collective-permute-start | bytes 884744 | tf_op jit(solution)/shard_map/ppermute | solution.py:35
  36.0 20.5 %copy-start.6 = (bf16[768,192]{0,1:T(8,128)(2,1)S(1)}, bf16[768,192]{0,1:T(8,128)(2,1)}, u32[]{:S(2)}) copy-start(bf16[768,192]{0,1:T(8,128)(2,1)} %get-tuple-element.24) | copy-start | bytes 884740
  36.0 20.5 %copy-start.7 = (bf16[768,192]{0,1:T(8,128)(2,1)S(1)}, bf16[768,192]{0,1:T(8,128)(2,1)}, u32[]{:S(2)}) copy-start(bf16[768,192]{0,1:T(8,128)(2,1)} %get-tuple-element.25) | copy-start | bytes 884740
  36.0 11.3 %collective-permute-start.6 = (bf16[768,192]{0,1:T(8,128)(2,1)}, bf16[768,192]{0,1:T(8,128)(2,1)}, u32[]{:S(2)}, u32[]{:S(2)}) collective-permute-start(bf16[768,192]{0,1:T(8,128)(2,1)} %get-tuple-element.23), channel_id=1, source_target_pairs={{0,4},{1,5},{2,6},{3,7},{4,0},{5,1},{6,2},{7,3},{8,12},{9,13},{10,... | collective-permute-start | bytes 884744 | tf_op jit(solution)/shard_map/ppermute | solution.py:35
  43.0 7.2 %collective-permute-start.3 = (bf16[192,768]{1,0:T(8,128)(2,1)S(1)}, bf16[192,768]{1,0:T(8,128)(2,1)S(1)}, u32[]{:S(2)}, u32[]{:S(2)}) collective-permute-start(bf16[192,768]{1,0:T(8,128)(2,1)S(1)} %broadcast_select_fusion.18), channel_id=1, source_target_pairs={{0,8},{1,9},{2,10},{3,11},{4,12},{5,13},{6,14},{7,15},{8,0},{9,1},... | collective-permute-start | bytes 884744 | tf_op jit(solution)/shard_map/ppermute | solution.py:35
  48.3 8.1 %collective-permute-start.7 = (bf16[768,192]{0,1:T(8,128)(2,1)S(1)}, bf16[768,192]{0,1:T(8,128)(2,1)S(1)}, u32[]{:S(2)}, u32[]{:S(2)}) collective-permute-start(bf16[768,192]{0,1:T(8,128)(2,1)S(1)} %broadcast_select_fusion.6), channel_id=1, source_target_pairs={{0,8},{1,9},{2,10},{3,11},{4,12},{5,13},{6,14},{7,15},{8,0},{9,1},... | collective-permute-start | bytes 884744 | tf_op jit(solution)/shard_map/ppermute | solution.py:35
  51.2 7.5 %copy-start.11 = (f32[1536]{0:T(1024)S(1)}, f32[1536]{0:T(1024)}, u32[]{:S(2)}) copy-start(f32[1536]{0:T(1024)} %param.13) | copy-start | bytes 18436
  57.5 10.7 %copy-start.10 = (f32[48,1536]{1,0:T(8,128)S(1)}, f32[48,1536]{1,0:T(8,128)}, u32[]{:S(2)}) copy-start(f32[48,1536]{1,0:T(8,128)} %param.17) | copy-start | bytes 884740
  60.8 15.3 %copy-start.2 = (f32[64,1536]{1,0:T(8,128)}, f32[64,1536]{1,0:T(8,128)S(1)}, u32[]{:S(2)}) copy-start(f32[64,1536]{1,0:T(8,128)S(1)} %get-tuple-element.40) | copy-start | bytes 1179652
  61.5 13.7 %all-to-all-start = ((f32[4,1,128]{2,1,0:T(1,128)}), f32[4,1,128]{2,1,0:T(1,128)S(1)}, u32[]{:S(2)}, u32[]{:S(2)}) async-start(f32[4,1,128]{2,1,0:T(1,128)} %broadcast_in_dim.6), calls=%async_computation | async-start | bytes 4096 | tf_op jit(solution)/shard_map/all_to_all | solution.py:11
  67.6 86.7 %all-gather.5.cloned.1.call-start = ((), (), s32[]{:S(2)}) async-start(), calls=%async_computation.6 | async-start | bytes 3342336 | tf_op jit(solution)/shard_map/all_gather | solution.py:158
  160.7 35.7 %all-to-all-start.1 = ((bf16[4,256,768]{2,1,0:T(8,128)(2,1)}), bf16[4,256,768]{2,1,0:T(8,128)(2,1)}, u32[]{:S(2)}, u32[]{:S(2)}) async-start(bf16[4,256,768]{2,1,0:T(8,128)(2,1)} %bitcast.54), calls=%async_computation.1 | async-start | bytes 3145728 | tf_op jit(solution)/shard_map/all_to_all | solution.py:59
  199.8 50.8 %copy-start.1 = (bf16[768,768]{0,1:T(8,128)(2,1)S(1)}, bf16[768,768]{0,1:T(8,128)(2,1)}, u32[]{:S(2)}) copy-start(bf16[768,768]{0,1:T(8,128)(2,1)} %get-tuple-element.27) | copy-start | bytes 3538948
  255.5 51.5 %all-to-all-start.3 = ((bf16[16,64,1536]{2,1,0:T(8,128)(2,1)}), bf16[16,64,1536]{2,1,0:T(8,128)(2,1)}, u32[]{:S(2)}, u32[]{:S(2)}) async-start(bf16[16,64,1536]{2,1,0:T(8,128)(2,1)} %bitcast.53), calls=%async_computation.3 | async-start | bytes 6291456 | tf_op jit(solution)/shard_map/all_to_all | solution.py:59
  307.0 2.4 copy-start.3
  311.0 10.8 %all-to-all-start.4 = ((f32[4,1,128]{2,1,0:T(1,128)}), f32[4,1,128]{2,1,0:T(1,128)S(1)}, u32[]{:S(2)}, u32[]{:S(2)}) async-start(f32[4,1,128]{2,1,0:T(1,128)} %broadcast_in_dim.8), calls=%async_computation.4 | async-start | bytes 4096 | tf_op jit(solution)/shard_map/all_to_all | solution.py:11
  317.1 4.8 %copy-start.8 = (f32[64,1536]{1,0:T(8,128)S(1)}, f32[64,1536]{1,0:T(8,128)}, u32[]{:S(2)}) copy-start(f32[64,1536]{1,0:T(8,128)} %get-tuple-element.19) | copy-start | bytes 1179652
  317.1 4.8 %copy-start.9 = (bf16[1536,128]{1,0:T(8,128)(2,1)S(1)}, bf16[1536,128]{1,0:T(8,128)(2,1)}, u32[]{:S(2)}) copy-start(bf16[1536,128]{1,0:T(8,128)(2,1)} %param.21) | copy-start | bytes 1179652
  317.1 4.8 %copy-start.12 = (f32[1536]{0:T(1024)S(1)}, f32[1536]{0:T(1024)}, u32[]{:S(2)}) copy-start(f32[1536]{0:T(1024)} %param.20) | copy-start | bytes 18436
Sparse Core Ops, SparseCore 0:
  58.8 56.1 all-gather.2
  116.8 37.4 all-gather.4
where the time goes:
time: 351 us; the launch traced here: 350 us
  waiting for transfers between devices  177 us (50%)
  blocking collectives  71.1 us (20%)
  starting transfers between devices  28.2 us (8%)
  other arithmetic  26.7 us (8%)
  matrix products  16.2 us (5%)
  local copies, waits for them, and re-layouts  15.9 us (5%)
  between operations  14.9 us (4%)
    all_to_all x2, waiting for transfers between devices, sent_and_summed(): parts = lax.all_to_all(cut_along(shard, dim, size), axis, 0, 0, tiled=True)  72.2 us
    all_to_all x1, blocking collectives, from_everyone(): lax.all_to_all(jnp.broadcast_to(shard[None], (size, *shard.shape)), axis,...  50.6 us
    all_gather x1, waiting for transfers between devices, rows_first(): out = lax.all_gather(both, axis, axis=0, tiled=True)  38.9 us
    all_gather x1, waiting for transfers between devices, on_device(): lax.all_gather(normed, 'col', axis=0, tiled=True)  34 us
    ppermute x8, waiting for transfers between devices, partner(): return lax.ppermute(value, axis, pairs)  24.3 us
    psum x1, blocking collectives, on_device(): lax.psum(jnp.dot(final_normed, check_weight, preferred_element_type=jnp.f...  20.5 us
    all_to_all x2, starting transfers between devices, sent_and_summed(): parts = lax.all_to_all(cut_along(shard, dim, size), axis, 0, 0, tiled=True)  12.7 us
    select_n x8, other arithmetic, move_halves(): jnp.where(upper_side, lower_part, upper_part)  11.2 us
  transfers between devices with their start and end apart: 14, of which 12 were waited for; matrix products, arithmetic and copies ran while one was open for 10% of the time, Pallas kernels for 0%

commit v1 on v0

--- a/solution.py
+++ b/solution.py
@@ -155,7 +155,9 @@
     embedded = jnp.dot(patches, embed_weight, preferred_element_type=jnp.float32) + embed_bias
     normed = norm_rows(embedded, layer_gain)
     partial_pre = jnp.dot(
-        lax.all_gather(normed, "col", axis=0, tiled=True),
+        jnp.concatenate(
+            lax.all_to_all(jnp.stack([normed] * lax.axis_size("col")), "col", 0, 0), axis=0
+        ),
         in_weight,
         preferred_element_type=jnp.float32,
     )

time: 351 us -> 325 us (0.926)
  waiting for transfers between devices: 177 us -> 154 us
  blocking collectives: 71.1 us -> 56.5 us
  starting transfers between devices: 28.2 us -> 37.9 us
    all_gather x1 -> x0, waiting for transfers between devices: 34 us -> none  [on_device(): lax.all_gather(normed, 'col', axis=0, tiled=True)]
    all_to_all x1, blocking collectives: 50.6 us -> 36 us  [from_everyone(): lax.all_to_all(jnp.broadcast_to(shard[None], (size, *shard.shape)), axis,...]
    all_to_all x2, waiting for transfers between devices: 72.2 us -> 83.1 us  [sent_and_summed(): parts = lax.all_to_all(cut_along(shard, dim, size), axis, 0, 0, tiled=True)]
    all_to_all x0 -> x1, waiting for transfers between devices: none -> 9.99 us  [on_device(): lax.all_to_all(jnp.stack([normed] * lax.axis_size('col')), 'col', 0, 0)]
    all_gather x1, waiting for transfers between devices: 38.9 us -> 29.8 us  [rows_first(): out = lax.all_gather(both, axis, axis=0, tiled=True)]
    all_to_all x0 -> x1, starting transfers between devices: none -> 7.74 us  [on_device(): lax.all_to_all(jnp.stack([normed] * lax.axis_size('col')), 'col', 0, 0)]
  transfers between devices with their start and end apart: 14 -> 14, of which waited for: 12 -> 12; matrix products, arithmetic and copies ran while one was open for 10% -> 11% of each run, Pallas kernels for 0% -> 0%
where the time goes in v1:
time: 325 us; the launch traced here: 324 us
  waiting for transfers between devices  154 us (47%)
  blocking collectives  56.5 us (17%)
  starting transfers between devices  37.9 us (12%)
  other arithmetic  26 us (8%)
  local copies, waits for them, and re-layouts  17.9 us (6%)
  matrix products  16.1 us (5%)
  between operations  14.9 us (5%)
    all_to_all x2, waiting for transfers between devices, sent_and_summed(): parts = lax.all_to_all(cut_along(shard, dim, size), axis, 0, 0, tiled=True)  83.1 us
    all_to_all x1, blocking collectives, from_everyone(): lax.all_to_all(jnp.broadcast_to(shard[None], (size, *shard.shape)), axis,...  36 us
    all_gather x1, waiting for transfers between devices, rows_first(): out = lax.all_gather(both, axis, axis=0, tiled=True)  29.8 us
    ppermute x8, waiting for transfers between devices, partner(): return lax.ppermute(value, axis, pairs)  24.3 us
    psum x1, blocking collectives, on_device(): lax.psum(jnp.dot(final_normed, check_weight, preferred_element_type=jnp.f...  20.5 us
    all_to_all x2, starting transfers between devices, sent_and_summed(): parts = lax.all_to_all(cut_along(shard, dim, size), axis, 0, 0, tiled=True)  14.7 us
    select_n x8, other arithmetic, move_halves(): jnp.where(upper_side, lower_part, upper_part)  11.2 us
    all_to_all x1, waiting for transfers between devices, on_device(): lax.all_to_all(jnp.stack([normed] * lax.axis_size('col')), 'col', 0, 0)  9.99 us
  transfers between devices with their start and end apart: 14, of which 12 were waited for; matrix products, arithmetic and copies ran while one was open for 11% of the time, Pallas kernels for 0%

profile of v1, /device:TPU:6, one launch (start us, length us, event | category | flops | bytes accessed | tf_op | source)
XLA Modules:
  0.0 323.7 jit_solution(3509081405633972241)
XLA Ops:
  7.2 1.6 copy-done
  9.6 2.5 constant_dynamic-slice_fusion
  12.1 1.1 copy.25
  13.3 1.2 copy.26
  15.7 1.7 broadcast_select_fusion.12
  18.2 1.7 broadcast_select_fusion.2
  20.0 1.2 collective-permute-start.5
  21.2 6.4 %collective-permute-done.1 = bf16[192,768]{1,0:T(8,128)(2,1)} collective-permute-done((bf16[192,768]{1,0:T(8,128)(2,1)}, bf16[192,768]{1,0:T(8,128)(2,1)}, u32[]{:S(2)}, u32[]{:S(2)}) %collective-permute-start.1) | collective-permute-done | bytes 294944 | tf_op jit(solution)/shard_map/ppermute | solution.py:35
  27.6 2.0 broadcast_select_fusion.15
  29.7 1.6 collective-permute-start.2
  31.3 2.6 collective-permute-done.5
  33.9 2.0 broadcast_select_fusion.5
  36.0 1.6 collective-permute-start.6
  37.6 4.3 %collective-permute-done.2 = bf16[192,768]{1,0:T(8,128)(2,1)} collective-permute-done((bf16[192,768]{1,0:T(8,128)(2,1)}, bf16[192,768]{1,0:T(8,128)(2,1)}, u32[]{:S(2)}, u32[]{:S(2)}) %collective-permute-start.2) | collective-permute-done | bytes 294944 | tf_op jit(solution)/shard_map/ppermute | solution.py:35
  41.9 1.1 broadcast_select_fusion.18
  43.1 4.2 %collective-permute-done.6 = bf16[768,192]{0,1:T(8,128)(2,1)} collective-permute-done((bf16[768,192]{0,1:T(8,128)(2,1)}, bf16[768,192]{0,1:T(8,128)(2,1)}, u32[]{:S(2)}, u32[]{:S(2)}) %collective-permute-start.6) | collective-permute-done | bytes 294944 | tf_op jit(solution)/shard_map/ppermute | solution.py:35
  47.2 1.1 broadcast_select_fusion.6
  48.6 1.5 collective-permute-done.3
  50.2 1.0 broadcast_select_fusion.17
  51.2 5.3 %collective-permute-done.7 = bf16[768,192]{0,1:T(8,128)(2,1)S(1)} collective-permute-done((bf16[768,192]{0,1:T(8,128)(2,1)S(1)}, bf16[768,192]{0,1:T(8,128)(2,1)S(1)}, u32[]{:S(2)}, u32[]{:S(2)}) %collective-permute-start.7) | collective-permute-done | bytes 294944 | tf_op jit(solution)/shard_map/ppermute | solution.py:35
  56.5 1.0 select_bitcast_fusion.1
  57.5 1.2 pad_maximum_fusion.2
  58.7 2.1 fusion.21
  61.5 6.1 %all-to-all-start = ((f32[4,1,128]{2,1,0:T(1,128)}), f32[4,1,128]{2,1,0:T(1,128)S(1)}, u32[]{:S(2)}, u32[]{:S(2)}) async-start(f32[4,1,128]{2,1,0:T(1,128)} %broadcast_in_dim.6), calls=%async_computation | async-start | bytes 4096 | tf_op jit(solution)/shard_map/all_to_all | solution.py:11
  68.5 6.7 %all-to-all-done = f32[4,1,128]{2,1,0:T(1,128)S(1)} async-done(((f32[4,1,128]{2,1,0:T(1,128)}), f32[4,1,128]{2,1,0:T(1,128)S(1)}, u32[]{:S(2)}, u32[]{:S(2)}) %all-to-all-start) | async-done | bytes 2080 | tf_op jit(solution)/shard_map/all_to_all | solution.py:11
  75.4 2.1 stack.2
  77.5 7.7 %all-to-all-start.1 = ((bf16[16,64,1536]{2,1,0:T(8,128)(2,1)}), bf16[16,64,1536]{2,1,0:T(8,128)(2,1)}, u32[]{:S(2)}, u32[]{:S(2)}) async-start(bf16[16,64,1536]{2,1,0:T(8,128)(2,1)} %stack.2), calls=%async_computation.1 | async-start | bytes 6291456 | tf_op jit(solution)/shard_map/all_to_all | solution.py:159
  85.2 29.8 %all-gather.2.cloned.1.call-done = bf16[768,3072]{1,0:T(8,128)(2,1)} async-done(((bf16[192,3072]{1,0:T(8,128)(2,1)}), bf16[768,3072]{1,0:T(8,128)(2,1)}) %all-gather.2.cloned.1.call-update) | async-done | bytes 4718608 | tf_op jit(solution)/shard_map/all_gather | solution.py:42
  115.0 3.7 %slice_bitcast_fusion.1 = (bf16[768,768]{0,1:T(8,128)(2,1)S(1)}, bf16[768,768]{0,1:T(8,128)(2,1)}, bf16[768,768]{1,0:T(8,128)(2,1)S(1)}, bf16[768,768]{1,0:T(8,128)(2,1)S(1)}) fusion(bf16[768,3072]{1,0:T(8,128)(2,1)} %all-gather.2.cloned.1.call-done), kind=kLoop, calls=%fused_computation.9 | loop fusion | bytes 9437184 | tf_op jit(solution)/shard_map/transpose | solution.py:46
  118.7 1.6 pad_maximum_fusion
  120.2 10.0 %all-to-all-done.1 = bf16[16,64,1536]{2,1,0:T(8,128)(2,1)} async-done(((bf16[16,64,1536]{2,1,0:T(8,128)(2,1)}), bf16[16,64,1536]{2,1,0:T(8,128)(2,1)}, u32[]{:S(2)}, u32[]{:S(2)}) %all-to-all-start.1) | async-done | bytes 3145760 | tf_op jit(solution)/shard_map/all_to_all | solution.py:159
  130.2 6.4 %convolution_convert_fusion.1 = bf16[1024,768]{1,0:T(8,128)(2,1)} fusion(bf16[1024,1536]{1,0:T(8,128)(2,1)} %bitcast.10, bf16[1536,768]{1,0:T(8,128)(2,1)} %pad_maximum_fusion), kind=kOutput, calls=%fused_computation.6 | convolution fusion | flops 2416705536 | bytes 7077888 | tf_op jit(solution)/shard_map/dot_general | solution.py:157
  136.6 4.5 %all-to-all-start.2 = ((bf16[4,256,768]{2,1,0:T(8,128)(2,1)}), bf16[4,256,768]{2,1,0:T(8,128)(2,1)}, u32[]{:S(2)}, u32[]{:S(2)}) async-start(bf16[4,256,768]{2,1,0:T(8,128)(2,1)} %bitcast.55), calls=%async_computation.2 | async-start | bytes 3145728 | tf_op jit(solution)/shard_map/all_to_all | solution.py:59
  141.1 1.1 convolution_reduce_fusion.2
  142.2 39.3 %all-to-all-done.2 = bf16[4,256,768]{2,1,0:T(8,128)(2,1)} async-done(((bf16[4,256,768]{2,1,0:T(8,128)(2,1)}), bf16[4,256,768]{2,1,0:T(8,128)(2,1)}, u32[]{:S(2)}, u32[]{:S(2)}) %all-to-all-start.2) | async-done | bytes 1572896 | tf_op jit(solution)/shard_map/all_to_all | solution.py:59
  181.6 1.7 convert_reduce_fusion.1
  183.3 1.7 fusion.2
  185.1 36.0 %all_to_all.32 = bf16[4,256,768]{2,1,0:T(8,128)(2,1)S(1)} all-to-all(bf16[4,256,768]{2,1,0:T(8,128)(2,1)S(1)} %broadcast_in_dim.7), channel_id=1, replica_groups=mesh['rep'=4,'row'=4,'col'=16] {'row'}, dimensions={0} | all-to-all | bytes 3145728 | tf_op jit(solution)/shard_map/all_to_all | solution.py:11
  221.1 4.9 %convolution_convert_fusion = bf16[1024,1536]{1,0:T(8,128)(2,1)} fusion(bf16[1024,768]{1,0:T(8,128)(2,1)S(1)} %bitcast.56, bf16[768,768]{0,1:T(8,128)(2,1)S(1)} %copy-done.1, bf16[768,768]{0,1:T(8,128)(2,1)S(1)} %get-tuple-element.26), kind=kOutput, calls=%fused_computation.1 | convolution fusion | flops 2422210560 | bytes 7077888 | tf_op jit(solution)/shard_map/dot_general | solution.py:166
  226.0 10.2 %all-to-all-start.4 = ((bf16[16,64,1536]{2,1,0:T(8,128)(2,1)}), bf16[16,64,1536]{2,1,0:T(8,128)(2,1)}, u32[]{:S(2)}, u32[]{:S(2)}) async-start(bf16[16,64,1536]{2,1,0:T(8,128)(2,1)} %bitcast.54), calls=%async_computation.4 | async-start | bytes 6291456 | tf_op jit(solution)/shard_map/all_to_all | solution.py:59
  236.2 1.2 convolution_reduce_fusion
  237.4 43.8 %all-to-all-done.4 = bf16[16,64,1536]{2,1,0:T(8,128)(2,1)} async-done(((bf16[16,64,1536]{2,1,0:T(8,128)(2,1)}), bf16[16,64,1536]{2,1,0:T(8,128)(2,1)}, u32[]{:S(2)}, u32[]{:S(2)}) %all-to-all-start.4) | async-done | bytes 3145760 | tf_op jit(solution)/shard_map/all_to_all | solution.py:59
  281.2 2.4 convert_reduce_fusion
  283.6 0.9 fusion.20
  285.2 3.2 all-to-all-start.5
  288.4 2.8 pad_maximum_fusion.1
  291.3 4.3 %copy.23 = bf16[768,1536]{1,0:T(8,128)(2,1)} copy(bf16[768,1536]{0,1:T(8,128)(2,1)} %pad_maximum_fusion.1) | data formatting | bytes 4718592
  296.4 20.5 %psum.7 = f32[64,128]{1,0:T(8,128)} all-reduce(f32[64,128]{1,0:T(8,128)S(1)} %fusion.10), channel_id=1, replica_groups=mesh['rep'=4,'row'=4,'col'=16] {'row'}, use_global_device_ids=true, to_apply=%region_8.9 | all-reduce | flops 8192 | bytes 65536 | tf_op jit(solution)/shard_map/psum | solution.py:171
  (50 shorter events, 6.1 us)
Async XLA Ops:
  7.2 1.7 copy-start
  7.2 107.8 %all-gather.2.cloned.1.call-start = ((), (), s32[]{:S(2)}) async-start(), calls=%async_computation.6 | async-start | bytes 5898240 | tf_op jit(solution)/shard_map/all_gather | solution.py:42
  9.6 6.1 %collective-permute-start = (bf16[192,768]{1,0:T(8,128)(2,1)}, bf16[192,768]{1,0:T(8,128)(2,1)}, u32[]{:S(2)}, u32[]{:S(2)}) collective-permute-start(bf16[192,768]{1,0:T(8,128)(2,1)} %broadcast_select_fusion.9), channel_id=1, source_target_pairs={{0,1},{1,0},{2,3},{3,2},{4,5},{5,4},{6,7},{7,6},{8,9},{9,8},{10,11... | collective-permute-start | bytes 884744 | tf_op jit(solution)/shard_map/ppermute | solution.py:35
  15.2 3.1 collective-permute-start.4
  17.4 10.2 %collective-permute-start.1 = (bf16[192,768]{1,0:T(8,128)(2,1)}, bf16[192,768]{1,0:T(8,128)(2,1)}, u32[]{:S(2)}, u32[]{:S(2)}) collective-permute-start(bf16[192,768]{1,0:T(8,128)(2,1)} %broadcast_select_fusion.12), channel_id=1, source_target_pairs={{0,2},{1,3},{2,0},{3,1},{4,6},{5,7},{6,4},{7,5},{8,10},{9,11},{10,... | collective-permute-start | bytes 884744 | tf_op jit(solution)/shard_map/ppermute | solution.py:35
  20.0 14.0 %collective-permute-start.5 = (bf16[768,192]{0,1:T(8,128)(2,1)}, bf16[768,192]{0,1:T(8,128)(2,1)}, u32[]{:S(2)}, u32[]{:S(2)}) collective-permute-start(bf16[768,192]{0,1:T(8,128)(2,1)} %broadcast_select_fusion.2), channel_id=1, source_target_pairs={{0,2},{1,3},{2,0},{3,1},{4,6},{5,7},{6,4},{7,5},{8,10},{9,11},{10,... | collective-permute-start | bytes 884744 | tf_op jit(solution)/shard_map/ppermute | solution.py:35
  29.7 20.5 %copy-start.4 = (bf16[192,768]{1,0:T(8,128)(2,1)S(1)}, bf16[192,768]{1,0:T(8,128)(2,1)}, u32[]{:S(2)}) copy-start(bf16[192,768]{1,0:T(8,128)(2,1)} %get-tuple-element.21) | copy-start | bytes 884740
  29.7 20.5 %copy-start.5 = (bf16[192,768]{1,0:T(8,128)(2,1)S(1)}, bf16[192,768]{1,0:T(8,128)(2,1)}, u32[]{:S(2)}) copy-start(bf16[192,768]{1,0:T(8,128)(2,1)} %get-tuple-element.22) | copy-start | bytes 884740
  29.7 12.2 %collective-permute-start.2 = (bf16[192,768]{1,0:T(8,128)(2,1)}, bf16[192,768]{1,0:T(8,128)(2,1)}, u32[]{:S(2)}, u32[]{:S(2)}) collective-permute-start(bf16[192,768]{1,0:T(8,128)(2,1)} %get-tuple-element.20), channel_id=1, source_target_pairs={{0,4},{1,5},{2,6},{3,7},{4,0},{5,1},{6,2},{7,3},{8,12},{9,13},{10,... | collective-permute-start | bytes 884744 | tf_op jit(solution)/shard_map/ppermute | solution.py:35
  36.0 20.5 %copy-start.6 = (bf16[768,192]{0,1:T(8,128)(2,1)S(1)}, bf16[768,192]{0,1:T(8,128)(2,1)}, u32[]{:S(2)}) copy-start(bf16[768,192]{0,1:T(8,128)(2,1)} %get-tuple-element.24) | copy-start | bytes 884740
  36.0 20.5 %copy-start.7 = (bf16[768,192]{0,1:T(8,128)(2,1)S(1)}, bf16[768,192]{0,1:T(8,128)(2,1)}, u32[]{:S(2)}) copy-start(bf16[768,192]{0,1:T(8,128)(2,1)} %get-tuple-element.25) | copy-start | bytes 884740
  36.0 11.3 %collective-permute-start.6 = (bf16[768,192]{0,1:T(8,128)(2,1)}, bf16[768,192]{0,1:T(8,128)(2,1)}, u32[]{:S(2)}, u32[]{:S(2)}) collective-permute-start(bf16[768,192]{0,1:T(8,128)(2,1)} %get-tuple-element.23), channel_id=1, source_target_pairs={{0,4},{1,5},{2,6},{3,7},{4,0},{5,1},{6,2},{7,3},{8,12},{9,13},{10,... | collective-permute-start | bytes 884744 | tf_op jit(solution)/shard_map/ppermute | solution.py:35
  43.0 7.2 %collective-permute-start.3 = (bf16[192,768]{1,0:T(8,128)(2,1)S(1)}, bf16[192,768]{1,0:T(8,128)(2,1)S(1)}, u32[]{:S(2)}, u32[]{:S(2)}) collective-permute-start(bf16[192,768]{1,0:T(8,128)(2,1)S(1)} %broadcast_select_fusion.18), channel_id=1, source_target_pairs={{0,8},{1,9},{2,10},{3,11},{4,12},{5,13},{6,14},{7,15},{8,0},{9,1},... | collective-permute-start | bytes 884744 | tf_op jit(solution)/shard_map/ppermute | solution.py:35
  48.3 8.1 %collective-permute-start.7 = (bf16[768,192]{0,1:T(8,128)(2,1)S(1)}, bf16[768,192]{0,1:T(8,128)(2,1)S(1)}, u32[]{:S(2)}, u32[]{:S(2)}) collective-permute-start(bf16[768,192]{0,1:T(8,128)(2,1)S(1)} %broadcast_select_fusion.6), channel_id=1, source_target_pairs={{0,8},{1,9},{2,10},{3,11},{4,12},{5,13},{6,14},{7,15},{8,0},{9,1},... | collective-permute-start | bytes 884744 | tf_op jit(solution)/shard_map/ppermute | solution.py:35
  51.2 7.5 %copy-start.11 = (f32[1536]{0:T(1024)S(1)}, f32[1536]{0:T(1024)}, u32[]{:S(2)}) copy-start(f32[1536]{0:T(1024)} %param.13) | copy-start | bytes 18436
  57.5 10.7 %copy-start.10 = (f32[48,1536]{1,0:T(8,128)S(1)}, f32[48,1536]{1,0:T(8,128)}, u32[]{:S(2)}) copy-start(f32[48,1536]{1,0:T(8,128)} %param.17) | copy-start | bytes 884740
  60.8 16.7 %copy-start.2 = (f32[64,1536]{1,0:T(8,128)}, f32[64,1536]{1,0:T(8,128)S(1)}, u32[]{:S(2)}) copy-start(f32[64,1536]{1,0:T(8,128)S(1)} %get-tuple-element.40) | copy-start | bytes 1179652
  61.5 13.7 %all-to-all-start = ((f32[4,1,128]{2,1,0:T(1,128)}), f32[4,1,128]{2,1,0:T(1,128)S(1)}, u32[]{:S(2)}, u32[]{:S(2)}) async-start(f32[4,1,128]{2,1,0:T(1,128)} %broadcast_in_dim.6), calls=%async_computation | async-start | bytes 4096 | tf_op jit(solution)/shard_map/all_to_all | solution.py:11
  77.5 52.7 %all-to-all-start.1 = ((bf16[16,64,1536]{2,1,0:T(8,128)(2,1)}), bf16[16,64,1536]{2,1,0:T(8,128)(2,1)}, u32[]{:S(2)}, u32[]{:S(2)}) async-start(bf16[16,64,1536]{2,1,0:T(8,128)(2,1)} %stack.2), calls=%async_computation.1 | async-start | bytes 6291456 | tf_op jit(solution)/shard_map/all_to_all | solution.py:159
  136.6 45.0 %all-to-all-start.2 = ((bf16[4,256,768]{2,1,0:T(8,128)(2,1)}), bf16[4,256,768]{2,1,0:T(8,128)(2,1)}, u32[]{:S(2)}, u32[]{:S(2)}) async-start(bf16[4,256,768]{2,1,0:T(8,128)(2,1)} %bitcast.55), calls=%async_computation.2 | async-start | bytes 3145728 | tf_op jit(solution)/shard_map/all_to_all | solution.py:59
  185.0 36.1 %copy-start.1 = (bf16[768,768]{0,1:T(8,128)(2,1)S(1)}, bf16[768,768]{0,1:T(8,128)(2,1)}, u32[]{:S(2)}) copy-start(bf16[768,768]{0,1:T(8,128)(2,1)} %get-tuple-element.27) | copy-start | bytes 3538948
  226.0 55.1 %all-to-all-start.4 = ((bf16[16,64,1536]{2,1,0:T(8,128)(2,1)}), bf16[16,64,1536]{2,1,0:T(8,128)(2,1)}, u32[]{:S(2)}, u32[]{:S(2)}) async-start(bf16[16,64,1536]{2,1,0:T(8,128)(2,1)} %bitcast.54), calls=%async_computation.4 | async-start | bytes 6291456 | tf_op jit(solution)/shard_map/all_to_all | solution.py:59
  281.2 2.4 copy-start.3
  285.2 10.8 %all-to-all-start.5 = ((f32[4,1,128]{2,1,0:T(1,128)}), f32[4,1,128]{2,1,0:T(1,128)S(1)}, u32[]{:S(2)}, u32[]{:S(2)}) async-start(f32[4,1,128]{2,1,0:T(1,128)} %broadcast_in_dim.8), calls=%async_computation.5 | async-start | bytes 4096 | tf_op jit(solution)/shard_map/all_to_all | solution.py:11
  291.3 4.8 %copy-start.8 = (f32[64,1536]{1,0:T(8,128)S(1)}, f32[64,1536]{1,0:T(8,128)}, u32[]{:S(2)}) copy-start(f32[64,1536]{1,0:T(8,128)} %get-tuple-element.19) | copy-start | bytes 1179652
  291.3 4.8 %copy-start.9 = (bf16[1536,128]{1,0:T(8,128)(2,1)S(1)}, bf16[1536,128]{1,0:T(8,128)(2,1)}, u32[]{:S(2)}) copy-start(bf16[1536,128]{1,0:T(8,128)(2,1)} %param.21) | copy-start | bytes 1179652
  291.3 4.8 %copy-start.12 = (f32[1536]{0:T(1024)S(1)}, f32[1536]{0:T(1024)}, u32[]{:S(2)}) copy-start(f32[1536]{0:T(1024)} %param.20) | copy-start | bytes 18436
Sparse Core Ops, SparseCore 0:
  58.8 56.1 all-gather.1
